TPU v7x, 32 devices: a whole 2x2x4 slice. The times are simulated.
32 devices in a mesh: wrow: 4 (over y, core), wcol: 2 (over x), dom: 4 (over z).
Axes of the slice: x: 2, y: 2, z: 4, core: 2. Of those that a mesh axis runs over, the one named last changes fastest.
Arguments:
- positions: float32 [4, 2, 3, 8192], P('wrow', 'wcol', None, 'dom'), may hold values from -6 to 6
- velocities: float32 [4, 2, 3, 8192], P('wrow', 'wcol', None, 'dom'), may hold values from -6 to 6
- inv_mass: float32 [8192], P('dom'), may hold values from 0.5 to 2
- cv_weight: float32 [2, 3, 8192], P(None, None, 'dom'), may hold values from -0.125 to 0.125
- stiffness: float32 [2], replicated, may hold values from 1 to 4
- centers: float32 [4, 2, 2], P('wrow', 'wcol'), may hold values from -3 to 3
- block_order: int32 [8192], P('dom'), may hold values from 0 to 2047, as said below
- pair_count: int32 [4], P('dom'), may hold values from 16 to 64, as said below
- pair_own: int32 [4, 64], P('dom'), may hold values from 0 to 15, as said below
- pair_other: int32 [4, 64], P('dom'), may hold values from 0 to 47, as said below
- accept_row: int32 [4, 2], P('wrow', 'wcol'), may hold values from 0 to 1, as said below
- accept_col: int32 [4, 2], P('wrow', 'wcol'), may hold values from 0 to 1, as said below
Outputs:
- new_positions: float32 [4, 2, 3, 8192], P('wrow', 'wcol', None, 'dom')
- new_velocities: float32 [4, 2, 3, 8192], P('wrow', 'wcol', None, 'dom')
- new_forces: float32 [4, 2, 3, 8192], P('wrow', 'wcol', None, 'dom')
Inputs may be any that keep to these rules, and one draw needn't show every extreme that they name: accept_row is equal for windows (2k, c) and (2k + 1, c). accept_col is equal for windows (r, 2k) and (r, 2k + 1). `block_order`: each slab's 2048 entries are a permutation of 0 to 2047. `pair_count`: some slab has exactly 64 live pairs. `pair_own`: entries past the slab's pair_count are 0. `pair_other`: slab 0 names no lower slab and the last slab no upper slab; entries past the slab's pair_count are 16.
All inputs are finite; a program needn't handle non-finite values.
Results may differ from a plain program's by a relative error of at most 0.0003.
Values sent between devices are 32-bit elements; how exact they have to be, the bound alone decides.
No kernel may reach another device: no remote copies, remote signals or barrier semaphores. Data moves between devices by JAX's collectives and lax.ppermute only.
A program may use at most 64 MiB of HBM per device.

v0:
```python
import functools
import math

import jax
import jax.numpy as jnp
from jax import lax
from jax.experimental import pallas as pl
from jax.experimental.pallas import tpu as pltpu
from jax.sharding import PartitionSpec as P

BLK = 128
STEPS = 3
PAIR_EPS = 0.015625
DT = 0.1
UNROLL = 16
PASS = 16
WIDE = 32
SMALL_VMEM = 4 << 20
MAIN_VMEM = 24 << 20
ROOT = math.sqrt(math.log2(math.e))


def rounded(x):
    return x.astype(jnp.bfloat16).astype(jnp.float32)


def lanes_from(source, low):
    return jnp.take_along_axis(source, low, axis=1, mode="promise_in_bounds")


def sub_row():
    return lax.broadcasted_iota(jnp.int32, (8, BLK), 0)


def is_fourth():
    row = sub_row()
    return (row == 3) | (row == 7)


def total4(value):
    value = value + pltpu.roll(value, 1, 0)
    return value + pltpu.roll(value, 2, 0)


def whole(value):
    return jnp.sum(jnp.sum(value, axis=0, keepdims=True), axis=1, keepdims=True)


def span(block):
    return pl.ds(pl.multiple_of(block * BLK, BLK), BLK)


def reordered(high, low, rows):
    found = []
    for b, group in enumerate(rows):
        here = high == b
        for k, row in enumerate(group):
            moved = lanes_from(jnp.broadcast_to(row, high.shape), low)
            if b:
                found[k] = jnp.where(here, moved, found[k])
            else:
                found.append(moved)
    return found


def state_kernel(blocks, centers, stiffness, pos, vel, mass, order, out):
    index = order[...]
    high, low = index // BLK, index % BLK
    refs = [(pos, 0), (pos, 1), (pos, 2), (mass, 0), (vel, 0), (vel, 1), (vel, 2)]
    rows = [
        [ref[k * blocks + b : k * blocks + b + 1, :] for ref, k in refs] for b in range(blocks)
    ]
    for k, value in enumerate(reordered(high, low, rows)):
        out[k * blocks : (k + 1) * blocks, :] = value
    lane = lax.broadcasted_iota(jnp.int32, (8, BLK), 1)
    aux = jnp.where(lane == 0, centers[0, 0], centers[0, 1])
    aux = jnp.where(lane == 2, stiffness[0], jnp.where(lane == 3, stiffness[1], aux))
    out[7 * blocks :, :] = aux


def weight_kernel(blocks, slots, count, cv, order, own, other, out, half):
    index = order[...]
    high, low = index // BLK, index % BLK
    rows = [
        [cv[pl.ds((c * blocks + b) * 2 + k, 1), :] for k in range(2) for c in range(3)]
        for b in range(blocks)
    ]
    odd = lax.rem(lax.axis_index("wrow"), 2) == 1
    found = reordered(high, low, rows)
    for k, value in enumerate(found):
        out[k * blocks : (k + 1) * blocks, :] = value
    for k in range(3):
        half[k * blocks : (k + 1) * blocks, :] = jnp.where(odd, found[k + 3], found[k])
    start = 6 * blocks
    out[start:, :] = jnp.zeros((out.shape[0] - start, BLK), jnp.float32) + count[0].astype(
        jnp.float32
    )
    lines = -(-slots // BLK)
    for j in range(lines):
        wide = min(BLK, slots - j * BLK)
        at = slice(j * BLK, j * BLK + wide)
        mine = start + 1 + j
        out[mine : mine + 1, 0:wide] = own[0:1, at].astype(jnp.float32)
        out[mine + lines : mine + lines + 1, 0:wide] = other[0:1, at].astype(jnp.float32)
    half[3 * blocks :, :] = out[start:, :]


def inverse_kernel(blocks, order, inv):
    size = blocks * BLK
    listed = jnp.concatenate([order[b : b + 1, :] for b in range(blocks)], 1)
    high, low = listed // BLK, listed % BLK
    place = lax.broadcasted_iota(jnp.int32, (blocks, size), 1)
    hit_high = lax.broadcasted_iota(jnp.int32, (blocks, size), 0) == high
    hit_low = lax.broadcasted_iota(jnp.int32, (BLK, size), 0) == low
    left = jnp.concatenate(
        [
            jnp.where(hit_high, place // BLK, 0).astype(jnp.float32),
            jnp.where(hit_high, place % BLK, 0).astype(jnp.float32),
        ],
        0,
    ).astype(jnp.bfloat16)
    right = jnp.where(hit_low, 1.0, 0.0).astype(jnp.bfloat16)
    inv[...] = lax.dot_general(
        left, right, (((1,), (1,)), ((), ())), preferred_element_type=jnp.float32
    ).astype(jnp.int32)


def by_xor(slabs):
    return slabs & (slabs - 1) == 0


def slab_of(me, slot, slabs):
    return me ^ slot if by_xor(slabs) else (me + slot) % slabs


def slot_of(slab, me, slabs):
    return slab ^ me if by_xor(slabs) else (slab - me + slabs) % slabs


class Pairs:
    def __init__(self, total, owners, others, acc, atab, ctab, htab, spread, parts):
        self.owners, self.others = owners, others
        self.acc, self.atab, self.ctab, self.htab = acc, atab, ctab, htab
        self.spread, self.parts = spread, parts
        atab[total] = jnp.zeros((32, BLK), jnp.bfloat16)
        parts[...] = jnp.zeros(parts.shape, jnp.float32)

    def tables(self, group):
        row, fourth = sub_row(), is_fourth()
        made = []
        for block, x in group:
            scaled = jnp.where(fourth, 0.0, x * ROOT)
            half = -0.5 * total4(scaled * scaled)
            base = jnp.where(fourth, half, scaled)
            s1 = rounded(base)
            rest = base - s1
            s2 = rounded(rest)
            s3 = rest - s2
            one = jnp.float32(1.0)
            zero = jnp.zeros_like(x)
            a0 = jnp.where(row == 7, s2, s1)
            a1 = jnp.where(row == 3, s3, jnp.where(row == 7, one, s2))
            a2 = jnp.where(row < 3, s1, jnp.where(fourth, one, s3))
            c0 = jnp.where(row < 3, s1, jnp.where(fourth, one, s2))
            c1 = jnp.where((row < 3) | (row == 7), s1, jnp.where(row == 3, one, s2))
            c2 = jnp.where((row < 3) | (row == 7), s3, jnp.where(row == 3, s2, s1))
            h0 = jnp.where(row == 3, one, jnp.where(row == 7, 0.0, jnp.where(row < 4, s1, s2)))
            h1 = jnp.where(row < 3, s3, 0.0)
            ours = jnp.concatenate([a0, a1, a2, zero], 0).astype(jnp.bfloat16)
            theirs = jnp.concatenate([c0, c1, c2, zero], 0).T.astype(jnp.bfloat16)
            heads = jnp.concatenate([h0, h1], 0).astype(jnp.bfloat16)
            made.append((block, ours, theirs, heads))
        for block, ours, theirs, heads in made:
            self.atab[block] = ours
            self.ctab[block] = theirs
            self.htab[block, :, :BLK] = heads
            self.htab[block, :, BLK:] = heads
            self.acc[block] = jnp.zeros((16, BLK), jnp.float32)

    def listed(self, refs, group):
        line, lane = group // (BLK // UNROLL), group % (BLK // UNROLL) * UNROLL
        return [[ref[line, lane + u] for u in range(UNROLL)] for ref in refs]

    def spreads(self, group):
        owners, others = self.listed([self.owners, self.others], group)
        return [
            jnp.dot(self.ctab[other], self.atab[own], preferred_element_type=jnp.float32)
            for own, other in zip(owners, others)
        ]

    def add(self, group):
        (owners,) = self.listed([self.owners], group)
        for u, own in enumerate(owners):
            self.acc[own] += self.parts[u]

    def run(self, limit):
        def some(group, _):
            later = self.spreads(group + 1)
            self.add(group - 1)
            new = []
            (others,) = self.listed([self.others], group)
            for u, other in enumerate(others):
                weight = jnp.exp2(jnp.minimum(self.spread[u], 0.0))
                upper = weight.astype(jnp.bfloat16)
                lower = (weight - upper.astype(jnp.float32)).astype(jnp.bfloat16)
                both = jnp.concatenate([upper, lower], 0)
                new.append(jnp.dot(self.htab[other], both, preferred_element_type=jnp.float32))
            for u in range(UNROLL):
                self.spread[u] = later[u]
            for u in range(UNROLL):
                self.parts[u] = new[u]
            return 0

        for u, value in enumerate(self.spreads(1)):
            self.spread[u] = value
        lax.fori_loop(1, limit + 1, some, 0)
        self.add(limit)
        self.parts[...] = jnp.zeros(self.parts.shape, jnp.float32)

    def force(self, got, x):
        fourth = is_fourth()
        moved = got[:8] + got[8:]
        moved = moved + pltpu.roll(moved, 4, 0)
        weight = total4(jnp.where(fourth, moved, 0.0))
        pair = (x * ROOT * weight - moved) * (PAIR_EPS / ROOT)
        return jnp.where(fourth, 0.0, pair)


def decode_kernel(slabs, blocks, slots, *refs):
    fixed_refs = refs[:slabs]
    counts, owners, others = refs[slabs:]
    me = lax.axis_index("dom").astype(jnp.int32)
    lines = -(-slots // BLK)
    total = slabs * blocks
    place = lax.broadcasted_iota(jnp.int32, owners.shape, 0) * BLK
    place = place + lax.broadcasted_iota(jnp.int32, owners.shape, 1) - UNROLL
    owner = jnp.full(owners.shape, total, jnp.int32)
    other = jnp.zeros(owners.shape, jnp.int32)
    start = jnp.zeros((1, BLK), jnp.int32)
    for slab in range(slabs):
        first = (3 if slab else 6) * blocks
        live = fixed_refs[slab][first : first + 1, :].astype(jnp.int32)
        for line in range(lines):
            at = first + 1 + line
            own = fixed_refs[slab][at : at + 1, :].astype(jnp.int32)
            q = fixed_refs[slab][at + lines : at + lines + 1, :].astype(jnp.int32)
            shift = jnp.where(q >= blocks, 1, 0) + jnp.where(q >= 2 * blocks, 1, 0)
            where = slot_of(slab_of(me, slab, slabs) + shift - 1, me, slabs)
            rank = place - start - line * BLK
            inside = (rank >= 0) & (rank < BLK) & (rank < live - line * BLK)
            rank = jnp.clip(rank, 0, BLK - 1)
            own = jnp.broadcast_to(own + slab * blocks, owners.shape)
            q = jnp.broadcast_to(q + (where - shift) * blocks, owners.shape)
            owner = jnp.where(inside, lanes_from(own, rank), owner)
            other = jnp.where(inside, lanes_from(q, rank), other)
        start = start + live
        if slab == 0:
            mine = (live + UNROLL - 1) // UNROLL
    owners[...] = owner
    others[...] = other
    lane = lax.broadcasted_iota(jnp.int32, (1, BLK), 1)
    counts[...] = jnp.where(lane == 0, mine, (start + UNROLL - 1) // UNROLL)


def steps_kernel(slabs, blocks, *refs):
    counts, owners, others, inv = refs[:4]
    state_refs = refs[4 : 4 + slabs]
    fixed_refs = refs[4 + slabs : 4 + 2 * slabs]
    twin_refs = [None, *refs[4 + 2 * slabs : 3 + 3 * slabs]]
    x_out, v_out, f_out = refs[3 + 3 * slabs : 6 + 3 * slabs]
    xs, vs, ms, w0s, w1s, packed, *rest = refs[6 + 3 * slabs :]
    odd = lax.rem(lax.axis_index("wrow"), 2) == 1
    acc = rest[0]
    total = slabs * blocks
    row, fourth = sub_row(), is_fourth()
    aux = state_refs[0][7 * blocks : 7 * blocks + 1, :]
    centre = [aux[:, k : k + 1] for k in range(2)]
    stiff = [aux[:, k : k + 1] for k in range(2, 4)]
    zero = jnp.zeros((8, BLK), jnp.float32)

    none = jnp.zeros((1, BLK), jnp.float32)

    def strided(ref, t, count):
        return ref[pl.ds(t, count, stride=blocks), :]

    work = Pairs(total, owners, others, *rest)

    sums = (zero, zero)
    for slab in range(slabs):

        def load(group, carry, slab=slab):
            done = []
            for u in range(PASS):
                t = group * PASS + u
                state = jnp.concatenate([strided(state_refs[slab], t, 7), none], 0)
                m = jnp.broadcast_to(state[3:4], (8, BLK))
                state = jnp.where(fourth, 0.0, state)
                turned = pltpu.roll(state, 4, 0)
                x = jnp.where(row < 4, state, turned)
                v = jnp.where(row < 4, turned, state)
                if slab:
                    mine = strided(fixed_refs[slab], t, 3)
                    twin = strided(twin_refs[slab], t, 3)
                else:
                    w = strided(fixed_refs[slab], t, 6)
                    mine, twin = w[:3], w[3:]
                w = jnp.concatenate([mine, none, twin, none], 0)
                turned = pltpu.roll(w, 4, 0)
                w0 = jnp.where(row < 4, w, turned)
                w1 = jnp.where(row < 4, turned, w)
                if slab:
                    w0, w1 = jnp.where(odd, w1, w0), jnp.where(odd, w0, w1)
                carry = carry[0] + w0 * x, carry[1] + w1 * x
                done.append((slab * blocks + t, x, v, m, w0, w1))
            for block, x, v, m, w0, w1 in done:
                xs[block] = x
                vs[block] = v
                ms[block] = m
                w0s[block] = w0
                w1s[block] = w1
            work.tables([(block, x) for block, x, *_ in done])
            return carry

        sums = lax.fori_loop(0, blocks // PASS, load, sums)

    def pulls(pair):
        return [stiff[k] * (0.5 * whole(pair[k]) - centre[k]) for k in range(2)]

    def step(number, sums):
        work.run(counts[0, 1])
        pull = pulls(sums)
        kick = jnp.where(number == 0, jnp.float32(0.5 * DT), jnp.float32(DT))

        def some(group, carry):
            moved = []
            for u in range(WIDE):
                block = group * WIDE + u
                x = xs[block]
                force = work.force(acc[block], x) - (pull[0] * w0s[block] + pull[1] * w1s[block])
                v = vs[block] + kick * ms[block] * force
                x = x + DT * v
                moved.append((block, x, v))
                carry = carry[0] + w0s[block] * x, carry[1] + w1s[block] * x
            for block, x, v in moved:
                xs[block] = x
                vs[block] = v
            work.tables([(block, x) for block, x, _ in moved])
            return carry

        return lax.fori_loop(0, total // WIDE, some, (zero, zero))

    sums = lax.fori_loop(0, STEPS, step, sums)
    work.run(counts[0, 0])
    pull = pulls(sums)

    for block in range(blocks):
        x = xs[block]
        force = work.force(acc[block], x) - (pull[0] * w0s[block] + pull[1] * w1s[block])
        v = vs[block] + (0.5 * DT) * ms[block] * force
        packed[block, 0:8] = jnp.where(row < 4, x, v)
        packed[block, 8:16] = force
    rows = [
        [packed[b, k : k + 1, :] for k in (0, 1, 2, 4, 5, 6, 8, 9, 10)] for b in range(blocks)
    ]
    found = reordered(inv[:blocks, :], inv[blocks:, :], rows)
    for k, value in enumerate(found):
        out = (x_out, v_out, f_out)[k // 3]
        k = k % 3
        out[k * blocks : (k + 1) * blocks, :] = value


def swapped(value, axis, accept):
    pairs = [(i, i ^ 1) for i in range(lax.axis_size(axis))]
    return jnp.where(accept == 1, lax.ppermute(value, axis, pairs), value)


def round_dom(value):
    count = lax.axis_size("dom")
    return [value] + [
        lax.ppermute(value, "dom", [(slab_of(i, s, count), i) for i in range(count)])
        for s in range(1, count)
    ]


def per_device(
    positions,
    velocities,
    inv_mass,
    cv_weight,
    stiffness,
    centers,
    block_order,
    pair_count,
    pair_own,
    pair_other,
    accept_row,
    accept_col,
):
    size = block_order.shape[0]
    blocks = size // BLK
    slots = pair_own.shape[1]
    slabs = lax.axis_size("dom")
    total = slabs * blocks
    vmem = pl.BlockSpec(memory_space=pltpu.VMEM)
    smem = pl.BlockSpec(memory_space=pltpu.SMEM)
    floats = jnp.float32
    tail = -(-(1 + 2 * -(-slots // BLK)) // 8) * 8

    def payload(count):
        return jax.ShapeDtypeStruct((count, BLK), floats)

    def lines(value):
        return value.reshape(-1, BLK)

    def small(flops):
        return dict(
            compiler_params=pltpu.CompilerParams(vmem_limit_bytes=SMALL_VMEM),
            cost_estimate=pl.CostEstimate(
                flops=flops, bytes_accessed=1 << 17, transcendentals=0
            ),
        )

    order = lines(block_order)
    state = pl.pallas_call(
        functools.partial(state_kernel, blocks),
        out_shape=payload(7 * blocks + 8),
        in_specs=[smem] * 2 + [vmem] * 4,
        out_specs=vmem,
    )(centers[0], stiffness, lines(positions), lines(velocities), lines(inv_mass), order)
    weights = cv_weight.reshape(2, 3, blocks, BLK).transpose(1, 2, 0, 3).reshape(-1, BLK)
    fixed, half = pl.pallas_call(
        functools.partial(weight_kernel, blocks, slots),
        out_shape=[payload(6 * blocks + tail), payload(3 * blocks + tail)],
        in_specs=[smem] + [vmem] * 4,
        out_specs=[vmem] * 2,
        **small(1 << 24),
    )(pair_count, weights, order, pair_own, pair_other)
    inverse = pl.pallas_call(
        functools.partial(inverse_kernel, blocks),
        out_shape=jax.ShapeDtypeStruct((2 * blocks, BLK), jnp.int32),
        in_specs=[vmem],
        out_specs=vmem,
        **small(1 << 24),
    )(order)

    state = swapped(state, "wrow", accept_row[0, 0])
    state = swapped(state, "wcol", accept_col[0, 0])
    fixeds = [fixed] + round_dom(half)[1:]
    states = round_dom(state)
    flips = [(i, i ^ 1) for i in range(lax.axis_size("wrow"))]
    twins = [lax.ppermute(value, "wrow", flips) for value in fixeds[1:]]

    room = -(-(slabs * slots + 4 * UNROLL) // (8 * BLK)) * 8
    tables = [(1, BLK)] + [(room, BLK)] * 2
    listed = pl.pallas_call(
        functools.partial(decode_kernel, slabs, blocks, slots),
        out_shape=[jax.ShapeDtypeStruct(shape, jnp.int32) for shape in tables],
        in_specs=[vmem] * slabs,
        out_specs=[vmem] * 3,
        **small(1 << 24),
    )(*fixeds)

    part = pltpu.VMEM((total, 8, BLK), floats)
    outs = pl.pallas_call(
        functools.partial(steps_kernel, slabs, blocks),
        out_shape=[jax.ShapeDtypeStruct((3 * blocks, BLK), floats)] * 3,
        in_specs=[smem] * 3 + [vmem] * (3 * slabs),
        out_specs=[vmem] * 3,
        scratch_shapes=[part] * 5
        + [
            pltpu.VMEM((blocks, 16, BLK), floats),
            pltpu.VMEM((total + 1, 16, BLK), floats),
            pltpu.VMEM((total + 1, 32, BLK), jnp.bfloat16),
            pltpu.VMEM((total, BLK, 32), jnp.bfloat16),
            pltpu.VMEM((total, 16, 2 * BLK), jnp.bfloat16),
            pltpu.VMEM((UNROLL, BLK, BLK), floats),
            pltpu.VMEM((UNROLL, 16, BLK), floats),
        ],
        compiler_params=pltpu.CompilerParams(vmem_limit_bytes=MAIN_VMEM),
    )(*listed, inverse, *states, *fixeds, *twins)
    return tuple(out.reshape(positions.shape) for out in outs)


def solution(mesh):
    placed = (
        P("wrow", "wcol", None, "dom"),
        P("wrow", "wcol", None, "dom"),
        P("dom"),
        P(None, None, "dom"),
        P(),
        P("wrow", "wcol", None),
        P("dom"),
        P("dom"),
        P("dom", None),
        P("dom", None),
        P("wrow", "wcol"),
        P("wrow", "wcol"),
    )
    return jax.shard_map(
        per_device,
        mesh=mesh,
        in_specs=placed,
        out_specs=(P("wrow", "wcol", None, "dom"),) * 3,
        check_vma=False,
    )
```

profile of v0, /device:TPU:0, one launch (start us, length us, event | category | flops | bytes accessed | tf_op | source)
XLA Modules:
  0.0 49.2 jit_solution(17064639701322763711)
XLA Ops:
  0.6 1.8 %shard_map.142 = f32[120,128]{1,0:T(8,128)} custom-call(f32[1,2]{1,0:T(1,128)} %bitcast.22, f32[2]{0:T(128)} %stiffness.1, f32[48,128]{1,0:T(8,128)} %bitcast.19, f32[48,128]{1,0:T(8,128)} %bitcast.20, f32[16,128]{1,0:T(8,128)} %bitcast.21, s32[16,128]{1,0:T(8,128)} %bitcast.15), custom_call_target="tpu_custom_call" | custom-call | tf_op jit(solution)/shard_map/pallas_call | solution.py:424
  2.4 0.5 %collective-permute-start.3 = (f32[120,128]{1,0:T(8,128)}, f32[120,128]{1,0:T(8,128)S(1)}, u32[]{:S(2)}, u32[]{:S(2)}) collective-permute-start(f32[120,128]{1,0:T(8,128)} %shard_map.142), channel_id=1, source_target_pairs={{0,8},{8,0},{16,24},{24,16},{1,9},{9,1},{17,25},{25,17},{2,10},{10... | collective-permute-start | bytes 184328 | tf_op jit(solution)/shard_map/ppermute | solution.py:374
  3.5 0.5 collective-permute-done.3
  4.0 0.0 copy-start
  4.0 0.0 copy-start.1
  4.0 3.7 %collective-permute-start.4 = (f32[120,128]{1,0:T(8,128)S(1)}, f32[120,128]{1,0:T(8,128)S(1)}, u32[]{:S(2)}, u32[]{:S(2)}) collective-permute-start(f32[120,128]{1,0:T(8,128)S(1)} %broadcast_select_fusion), channel_id=1, source_target_pairs={{0,4},{4,0},{1,5},{5,1},{2,6},{6,2},{3,7},{7,3},{8,12},{12,8},{9,1... | collective-permute-start | bytes 184328 | tf_op jit(solution)/shard_map/ppermute | solution.py:374
  8.3 0.0 copy-start.2
  8.3 0.0 copy-start.3
  8.4 0.0 copy-done
  8.4 0.0 copy-done.1
  8.4 0.6 %copy-done.2 = s32[1,64]{1,0:T(1,128)S(1)} copy-done((s32[1,64]{1,0:T(1,128)S(1)}, s32[1,64]{1,0:T(1,128)}, u32[]{:S(2)}) %copy-start.2) | copy-done | bytes 280
  9.0 0.0 copy-done.3
  9.0 0.3 shard_map.139
  9.3 3.7 %collective-permute-start.2 = (f32[56,128]{1,0:T(8,128)S(1)}, f32[56,128]{1,0:T(8,128)S(1)}, u32[]{:S(2)}, u32[]{:S(2)}) collective-permute-start(f32[56,128]{1,0:T(8,128)S(1)} %get-tuple-element.12), channel_id=1, source_target_pairs={{3,0},{2,1},{1,2},{0,3},{7,4},{6,5},{5,6},{4,7},{11,8},{10,9},{9,1... | collective-permute-start | bytes 86024 | tf_op jit(solution)/shard_map/ppermute | solution.py:380
  13.0 0.0 collective-permute-start.1
  13.6 0.0 collective-permute-done.4
  13.6 2.0 %collective-permute-start.7 = (f32[120,128]{1,0:T(8,128)S(1)}, f32[120,128]{1,0:T(8,128)S(1)}, u32[]{:S(2)}, u32[]{:S(2)}) collective-permute-start(f32[120,128]{1,0:T(8,128)S(1)} %broadcast_select_fusion.1.refs_4_), channel_id=1, source_target_pairs={{3,0},{2,1},{1,2},{0,3},{7,4},{6,5},{5,6},{4,7},{11,8},{10,9},{9,1... | collective-permute-start | bytes 184328 | tf_op jit(solution)/shard_map/ppermute | solution.py:380
  15.6 1.1 %collective-permute-start.6 = (f32[120,128]{1,0:T(8,128)S(1)}, f32[120,128]{1,0:T(8,128)S(1)}, u32[]{:S(2)}, u32[]{:S(2)}) collective-permute-start(f32[120,128]{1,0:T(8,128)S(1)} %broadcast_select_fusion.1.refs_4_), channel_id=1, source_target_pairs={{2,0},{3,1},{0,2},{1,3},{6,4},{7,5},{4,6},{5,7},{10,8},{11,9},{8,1... | collective-permute-start | bytes 184328 | tf_op jit(solution)/shard_map/ppermute | solution.py:380
  16.7 1.4 %collective-permute-start.5 = (f32[120,128]{1,0:T(8,128)S(1)}, f32[120,128]{1,0:T(8,128)S(1)}, u32[]{:S(2)}, u32[]{:S(2)}) collective-permute-start(f32[120,128]{1,0:T(8,128)S(1)} %broadcast_select_fusion.1.refs_4_), channel_id=1, source_target_pairs={{1,0},{0,1},{3,2},{2,3},{5,4},{4,5},{7,6},{6,7},{9,8},{8,9},{11,10... | collective-permute-start | bytes 184328 | tf_op jit(solution)/shard_map/ppermute | solution.py:380
  18.1 0.0 collective-permute-done.2.refs_3_.refs_11_
  18.1 0.6 %collective-permute-start = (f32[56,128]{1,0:T(8,128)S(1)}, f32[56,128]{1,0:T(8,128)S(1)}, u32[]{:S(2)}, u32[]{:S(2)}) collective-permute-start(f32[56,128]{1,0:T(8,128)S(1)} %get-tuple-element.12), channel_id=1, source_target_pairs={{1,0},{0,1},{3,2},{2,3},{5,4},{4,5},{7,6},{6,7},{9,8},{8,9},{11,10... | collective-permute-start | bytes 86024 | tf_op jit(solution)/shard_map/ppermute | solution.py:380
  18.7 0.0 collective-permute-done.1.refs_2_.refs_10_
  18.7 0.0 collective-permute-start.10
  18.8 3.4 %collective-permute-done.refs_1_.refs_9_ = f32[56,128]{1,0:T(8,128)S(1)} collective-permute-done((f32[56,128]{1,0:T(8,128)S(1)}, f32[56,128]{1,0:T(8,128)S(1)}, u32[]{:S(2)}, u32[]{:S(2)}) %collective-permute-start) | collective-permute-done | bytes 28704 | tf_op jit(solution)/shard_map/ppermute | solution.py:380
  22.1 0.0 collective-permute-start.9
  22.1 0.0 collective-permute-done.10.refs_14_
  22.1 0.5 %collective-permute-start.8 = (f32[56,128]{1,0:T(8,128)S(1)}, f32[56,128]{1,0:T(8,128)S(1)}, u32[]{:S(2)}, u32[]{:S(2)}) collective-permute-start(f32[56,128]{1,0:T(8,128)S(1)} %collective-permute-done.refs_1_.refs_9_), channel_id=1, source_target_pairs={{0,8},{8,0},{16,24},{24,16},{1,9},{9,1},{17,25},{25,17},{2,10},{10... | collective-permute-start | bytes 86024 | tf_op jit(solution)/shard_map/ppermute | solution.py:451
  22.6 0.3 shard_map.141.refs_3_
  22.9 0.1 shard_map.140
  23.0 0.3 collective-permute-done.9.refs_13_
  23.3 0.2 collective-permute-done.8.refs_12_
  23.5 0.0 collective-permute-done.7.refs_7_
  23.5 0.0 collective-permute-done.6.refs_6_
  23.5 0.0 collective-permute-done.5.refs_5_
  23.5 25.7 %shard_map.143 = (f32[48,128]{1,0:T(8,128)}, f32[48,128]{1,0:T(8,128)}, f32[48,128]{1,0:T(8,128)}) custom-call(s32[1,128]{1,0:T(1,128)S(1)} %get-tuple-element.13.refs_0_, s32[8,128]{1,0:T(8,128)S(1)} %get-tuple-element.14.refs_1_, s32[8,128]{1,0:T(8,128)S(1)} %get-tuple-element.15.refs_2_, s32[32,128]{1,0:T(8,128)S(1)} %shard_map.141.refs_3_, ...), custom_call_target="tpu_custom_call" | custom-call | tf_op jit(solution)/shard_map/pallas_call | solution.py:464
  (2 shorter events, 0.0 us)
Async XLA Ops:
  2.4 1.6 %collective-permute-start.3 = (f32[120,128]{1,0:T(8,128)}, f32[120,128]{1,0:T(8,128)S(1)}, u32[]{:S(2)}, u32[]{:S(2)}) collective-permute-start(f32[120,128]{1,0:T(8,128)} %shard_map.142), channel_id=1, source_target_pairs={{0,8},{8,0},{16,24},{24,16},{1,9},{9,1},{17,25},{25,17},{2,10},{10... | collective-permute-start | bytes 184328 | tf_op jit(solution)/shard_map/ppermute | solution.py:374
  4.0 4.4 %copy-start = (s32[2048]{0:T(1024)S(1)}, s32[2048]{0:T(1024)}, u32[]{:S(2)}) copy-start(s32[2048]{0:T(1024)} %param.18) | copy-start | bytes 24580
  4.0 4.4 %copy-start.1 = (f32[2,3,2048]{2,0,1:T(2,128)S(1)}, f32[2,3,2048]{2,0,1:T(2,128)}, u32[]{:S(2)}) copy-start(f32[2,3,2048]{2,0,1:T(2,128)} %param.15) | copy-start | bytes 147460
  4.0 9.6 %collective-permute-start.4 = (f32[120,128]{1,0:T(8,128)S(1)}, f32[120,128]{1,0:T(8,128)S(1)}, u32[]{:S(2)}, u32[]{:S(2)}) collective-permute-start(f32[120,128]{1,0:T(8,128)S(1)} %broadcast_select_fusion), channel_id=1, source_target_pairs={{0,4},{4,0},{1,5},{5,1},{2,6},{6,2},{3,7},{7,3},{8,12},{12,8},{9,1... | collective-permute-start | bytes 184328 | tf_op jit(solution)/shard_map/ppermute | solution.py:374
  8.3 0.7 %copy-start.2 = (s32[1,64]{1,0:T(1,128)S(1)}, s32[1,64]{1,0:T(1,128)}, u32[]{:S(2)}) copy-start(s32[1,64]{1,0:T(1,128)} %own.1) | copy-start | bytes 772
  8.3 0.7 %copy-start.3 = (s32[1,64]{1,0:T(1,128)S(1)}, s32[1,64]{1,0:T(1,128)}, u32[]{:S(2)}) copy-start(s32[1,64]{1,0:T(1,128)} %other.1) | copy-start | bytes 772
  9.3 8.8 %collective-permute-start.2 = (f32[56,128]{1,0:T(8,128)S(1)}, f32[56,128]{1,0:T(8,128)S(1)}, u32[]{:S(2)}, u32[]{:S(2)}) collective-permute-start(f32[56,128]{1,0:T(8,128)S(1)} %get-tuple-element.12), channel_id=1, source_target_pairs={{3,0},{2,1},{1,2},{0,3},{7,4},{6,5},{5,6},{4,7},{11,8},{10,9},{9,1... | collective-permute-start | bytes 86024 | tf_op jit(solution)/shard_map/ppermute | solution.py:380
  13.0 5.8 %collective-permute-start.1 = (f32[56,128]{1,0:T(8,128)S(1)}, f32[56,128]{1,0:T(8,128)S(1)}, u32[]{:S(2)}, u32[]{:S(2)}) collective-permute-start(f32[56,128]{1,0:T(8,128)S(1)} %get-tuple-element.12), channel_id=1, source_target_pairs={{2,0},{3,1},{0,2},{1,3},{6,4},{7,5},{4,6},{5,7},{10,8},{11,9},{8,1... | collective-permute-start | bytes 86024 | tf_op jit(solution)/shard_map/ppermute | solution.py:380
  13.6 9.8 %collective-permute-start.7 = (f32[120,128]{1,0:T(8,128)S(1)}, f32[120,128]{1,0:T(8,128)S(1)}, u32[]{:S(2)}, u32[]{:S(2)}) collective-permute-start(f32[120,128]{1,0:T(8,128)S(1)} %broadcast_select_fusion.1.refs_4_), channel_id=1, source_target_pairs={{3,0},{2,1},{1,2},{0,3},{7,4},{6,5},{5,6},{4,7},{11,8},{10,9},{9,1... | collective-permute-start | bytes 184328 | tf_op jit(solution)/shard_map/ppermute | solution.py:380
  15.6 7.9 %collective-permute-start.6 = (f32[120,128]{1,0:T(8,128)S(1)}, f32[120,128]{1,0:T(8,128)S(1)}, u32[]{:S(2)}, u32[]{:S(2)}) collective-permute-start(f32[120,128]{1,0:T(8,128)S(1)} %broadcast_select_fusion.1.refs_4_), channel_id=1, source_target_pairs={{2,0},{3,1},{0,2},{1,3},{6,4},{7,5},{4,6},{5,7},{10,8},{11,9},{8,1... | collective-permute-start | bytes 184328 | tf_op jit(solution)/shard_map/ppermute | solution.py:380
  16.7 6.8 %collective-permute-start.5 = (f32[120,128]{1,0:T(8,128)S(1)}, f32[120,128]{1,0:T(8,128)S(1)}, u32[]{:S(2)}, u32[]{:S(2)}) collective-permute-start(f32[120,128]{1,0:T(8,128)S(1)} %broadcast_select_fusion.1.refs_4_), channel_id=1, source_target_pairs={{1,0},{0,1},{3,2},{2,3},{5,4},{4,5},{7,6},{6,7},{9,8},{8,9},{11,10... | collective-permute-start | bytes 184328 | tf_op jit(solution)/shard_map/ppermute | solution.py:380
  18.1 4.0 %collective-permute-start = (f32[56,128]{1,0:T(8,128)S(1)}, f32[56,128]{1,0:T(8,128)S(1)}, u32[]{:S(2)}, u32[]{:S(2)}) collective-permute-start(f32[56,128]{1,0:T(8,128)S(1)} %get-tuple-element.12), channel_id=1, source_target_pairs={{1,0},{0,1},{3,2},{2,3},{5,4},{4,5},{7,6},{6,7},{9,8},{8,9},{11,10... | collective-permute-start | bytes 86024 | tf_op jit(solution)/shard_map/ppermute | solution.py:380
  18.7 3.4 %collective-permute-start.10 = (f32[56,128]{1,0:T(8,128)S(1)}, f32[56,128]{1,0:T(8,128)S(1)}, u32[]{:S(2)}, u32[]{:S(2)}) collective-permute-start(f32[56,128]{1,0:T(8,128)S(1)} %collective-permute-done.2.refs_3_.refs_11_), channel_id=1, source_target_pairs={{0,8},{8,0},{16,24},{24,16},{1,9},{9,1},{17,25},{25,17},{2,10},{10... | collective-permute-start | bytes 86024 | tf_op jit(solution)/shard_map/ppermute | solution.py:451
  22.1 1.2 %collective-permute-start.9 = (f32[56,128]{1,0:T(8,128)S(1)}, f32[56,128]{1,0:T(8,128)S(1)}, u32[]{:S(2)}, u32[]{:S(2)}) collective-permute-start(f32[56,128]{1,0:T(8,128)S(1)} %collective-permute-done.1.refs_2_.refs_10_), channel_id=1, source_target_pairs={{0,8},{8,0},{16,24},{24,16},{1,9},{9,1},{17,25},{25,17},{2,10},{10... | collective-permute-start | bytes 86024 | tf_op jit(solution)/shard_map/ppermute | solution.py:451
  22.1 1.4 %collective-permute-start.8 = (f32[56,128]{1,0:T(8,128)S(1)}, f32[56,128]{1,0:T(8,128)S(1)}, u32[]{:S(2)}, u32[]{:S(2)}) collective-permute-start(f32[56,128]{1,0:T(8,128)S(1)} %collective-permute-done.refs_1_.refs_9_), channel_id=1, source_target_pairs={{0,8},{8,0},{16,24},{24,16},{1,9},{9,1},{17,25},{25,17},{2,10},{10... | collective-permute-start | bytes 86024 | tf_op jit(solution)/shard_map/ppermute | solution.py:451
where the time goes:
time: 49 us; the launch traced here: 49.2 us
  Pallas kernels  28.1 us (57%)
  starting transfers between devices  13.4 us (27%)
  waiting for transfers between devices  4.31 us (9%)
  between operations  2.66 us (5%)
  local copies, waits for them, and re-layouts  0.65 us (1%)
    pallas_call x1, Pallas kernels, per_device(): pl.pallas_call(functools.partial(steps_kernel, slabs, blocks), out_shape=...  25.7 us
    ppermute x6, starting transfers between devices, round_dom(): lax.ppermute(value, 'dom', [(slab_of(i, s, count), i) for i in range(coun...  8.76 us
    ppermute x2, starting transfers between devices, swapped(): return jnp.where(accept == 1, lax.ppermute(value, axis, pairs), value)  4.16 us
    ppermute x6, waiting for transfers between devices, round_dom(): lax.ppermute(value, 'dom', [(slab_of(i, s, count), i) for i in range(coun...  3.38 us
    pallas_call x1, Pallas kernels, per_device(): pl.pallas_call(functools.partial(state_kernel, blocks), out_shape=payload...  1.76 us
  transfers between devices with their start and end apart: 11, of which 4 were waited for; matrix products, arithmetic and copies ran while one was open for 0% of the time, Pallas kernels for 1%

commit v1 on v0

--- a/solution.py
+++ b/solution.py
@@ -14,7 +14,7 @@
 DT = 0.1
 UNROLL = 16
 PASS = 16
-WIDE = 32
+WIDE = 64
 SMALL_VMEM = 4 << 20
 MAIN_VMEM = 24 << 20
 ROOT = math.sqrt(math.log2(math.e))

time: 49 us -> 48.9 us (level)
  Pallas kernels: 28.1 us -> 27.6 us
    pallas_call x1, Pallas kernels: 25.7 us -> 25.2 us  [per_device(): pl.pallas_call(functools.partial(steps_kernel, slabs, blocks), out_shape=...]
where the time goes in v1:
time: 48.9 us; the launch traced here: 48.7 us
  Pallas kernels  27.6 us (56%)
  starting transfers between devices  13.4 us (27%)
  waiting for transfers between devices  4.31 us (9%)
  between operations  2.66 us (5%)
  local copies, waits for them, and re-layouts  0.65 us (1%)
    pallas_call x1, Pallas kernels, per_device(): pl.pallas_call(functools.partial(steps_kernel, slabs, blocks), out_shape=...  25.2 us
    ppermute x6, starting transfers between devices, round_dom(): lax.ppermute(value, 'dom', [(slab_of(i, s, count), i) for i in range(coun...  8.76 us
    ppermute x2, starting transfers between devices, swapped(): return jnp.where(accept == 1, lax.ppermute(value, axis, pairs), value)  4.16 us
    ppermute x6, waiting for transfers between devices, round_dom(): lax.ppermute(value, 'dom', [(slab_of(i, s, count), i) for i in range(coun...  3.38 us
    pallas_call x1, Pallas kernels, per_device(): pl.pallas_call(functools.partial(state_kernel, blocks), out_shape=payload...  1.76 us
  transfers between devices with their start and end apart: 11, of which 4 were waited for; matrix products, arithmetic and copies ran while one was open for 0% of the time, Pallas kernels for 1%

profile of v1, /device:TPU:0, one launch (start us, length us, event | category | flops | bytes accessed | tf_op | source)
XLA Modules:
  0.0 48.7 jit_solution(10587690487327327172)
XLA Ops:
  0.6 1.8 %shard_map.142 = f32[120,128]{1,0:T(8,128)} custom-call(f32[1,2]{1,0:T(1,128)} %bitcast.22, f32[2]{0:T(128)} %stiffness.1, f32[48,128]{1,0:T(8,128)} %bitcast.19, f32[48,128]{1,0:T(8,128)} %bitcast.20, f32[16,128]{1,0:T(8,128)} %bitcast.21, s32[16,128]{1,0:T(8,128)} %bitcast.15), custom_call_target="tpu_custom_call" | custom-call | tf_op jit(solution)/shard_map/pallas_call | solution.py:424
  2.4 0.5 %collective-permute-start.3 = (f32[120,128]{1,0:T(8,128)}, f32[120,128]{1,0:T(8,128)S(1)}, u32[]{:S(2)}, u32[]{:S(2)}) collective-permute-start(f32[120,128]{1,0:T(8,128)} %shard_map.142), channel_id=1, source_target_pairs={{0,8},{8,0},{16,24},{24,16},{1,9},{9,1},{17,25},{25,17},{2,10},{10... | collective-permute-start | bytes 184328 | tf_op jit(solution)/shard_map/ppermute | solution.py:374
  3.5 0.5 collective-permute-done.3
  4.0 0.0 copy-start
  4.0 0.0 copy-start.1
  4.0 3.7 %collective-permute-start.4 = (f32[120,128]{1,0:T(8,128)S(1)}, f32[120,128]{1,0:T(8,128)S(1)}, u32[]{:S(2)}, u32[]{:S(2)}) collective-permute-start(f32[120,128]{1,0:T(8,128)S(1)} %broadcast_select_fusion), channel_id=1, source_target_pairs={{0,4},{4,0},{1,5},{5,1},{2,6},{6,2},{3,7},{7,3},{8,12},{12,8},{9,1... | collective-permute-start | bytes 184328 | tf_op jit(solution)/shard_map/ppermute | solution.py:374
  8.3 0.0 copy-start.2
  8.3 0.0 copy-start.3
  8.4 0.0 copy-done
  8.4 0.0 copy-done.1
  8.4 0.6 %copy-done.2 = s32[1,64]{1,0:T(1,128)S(1)} copy-done((s32[1,64]{1,0:T(1,128)S(1)}, s32[1,64]{1,0:T(1,128)}, u32[]{:S(2)}) %copy-start.2) | copy-done | bytes 280
  9.0 0.0 copy-done.3
  9.0 0.3 shard_map.139
  9.3 3.7 %collective-permute-start.2 = (f32[56,128]{1,0:T(8,128)S(1)}, f32[56,128]{1,0:T(8,128)S(1)}, u32[]{:S(2)}, u32[]{:S(2)}) collective-permute-start(f32[56,128]{1,0:T(8,128)S(1)} %get-tuple-element.12), channel_id=1, source_target_pairs={{3,0},{2,1},{1,2},{0,3},{7,4},{6,5},{5,6},{4,7},{11,8},{10,9},{9,1... | collective-permute-start | bytes 86024 | tf_op jit(solution)/shard_map/ppermute | solution.py:380
  13.0 0.0 collective-permute-start.1
  13.6 0.0 collective-permute-done.4
  13.6 2.0 %collective-permute-start.7 = (f32[120,128]{1,0:T(8,128)S(1)}, f32[120,128]{1,0:T(8,128)S(1)}, u32[]{:S(2)}, u32[]{:S(2)}) collective-permute-start(f32[120,128]{1,0:T(8,128)S(1)} %broadcast_select_fusion.1.refs_4_), channel_id=1, source_target_pairs={{3,0},{2,1},{1,2},{0,3},{7,4},{6,5},{5,6},{4,7},{11,8},{10,9},{9,1... | collective-permute-start | bytes 184328 | tf_op jit(solution)/shard_map/ppermute | solution.py:380
  15.6 1.1 %collective-permute-start.6 = (f32[120,128]{1,0:T(8,128)S(1)}, f32[120,128]{1,0:T(8,128)S(1)}, u32[]{:S(2)}, u32[]{:S(2)}) collective-permute-start(f32[120,128]{1,0:T(8,128)S(1)} %broadcast_select_fusion.1.refs_4_), channel_id=1, source_target_pairs={{2,0},{3,1},{0,2},{1,3},{6,4},{7,5},{4,6},{5,7},{10,8},{11,9},{8,1... | collective-permute-start | bytes 184328 | tf_op jit(solution)/shard_map/ppermute | solution.py:380
  16.7 1.4 %collective-permute-start.5 = (f32[120,128]{1,0:T(8,128)S(1)}, f32[120,128]{1,0:T(8,128)S(1)}, u32[]{:S(2)}, u32[]{:S(2)}) collective-permute-start(f32[120,128]{1,0:T(8,128)S(1)} %broadcast_select_fusion.1.refs_4_), channel_id=1, source_target_pairs={{1,0},{0,1},{3,2},{2,3},{5,4},{4,5},{7,6},{6,7},{9,8},{8,9},{11,10... | collective-permute-start | bytes 184328 | tf_op jit(solution)/shard_map/ppermute | solution.py:380
  18.1 0.0 collective-permute-done.2.refs_3_.refs_11_
  18.1 0.6 %collective-permute-start = (f32[56,128]{1,0:T(8,128)S(1)}, f32[56,128]{1,0:T(8,128)S(1)}, u32[]{:S(2)}, u32[]{:S(2)}) collective-permute-start(f32[56,128]{1,0:T(8,128)S(1)} %get-tuple-element.12), channel_id=1, source_target_pairs={{1,0},{0,1},{3,2},{2,3},{5,4},{4,5},{7,6},{6,7},{9,8},{8,9},{11,10... | collective-permute-start | bytes 86024 | tf_op jit(solution)/shard_map/ppermute | solution.py:380
  18.7 0.0 collective-permute-done.1.refs_2_.refs_10_
  18.7 0.0 collective-permute-start.10
  18.8 3.4 %collective-permute-done.refs_1_.refs_9_ = f32[56,128]{1,0:T(8,128)S(1)} collective-permute-done((f32[56,128]{1,0:T(8,128)S(1)}, f32[56,128]{1,0:T(8,128)S(1)}, u32[]{:S(2)}, u32[]{:S(2)}) %collective-permute-start) | collective-permute-done | bytes 28704 | tf_op jit(solution)/shard_map/ppermute | solution.py:380
  22.1 0.0 collective-permute-start.9
  22.1 0.0 collective-permute-done.10.refs_14_
  22.1 0.5 %collective-permute-start.8 = (f32[56,128]{1,0:T(8,128)S(1)}, f32[56,128]{1,0:T(8,128)S(1)}, u32[]{:S(2)}, u32[]{:S(2)}) collective-permute-start(f32[56,128]{1,0:T(8,128)S(1)} %collective-permute-done.refs_1_.refs_9_), channel_id=1, source_target_pairs={{0,8},{8,0},{16,24},{24,16},{1,9},{9,1},{17,25},{25,17},{2,10},{10... | collective-permute-start | bytes 86024 | tf_op jit(solution)/shard_map/ppermute | solution.py:451
  22.6 0.3 shard_map.141.refs_3_
  22.9 0.1 shard_map.140
  23.0 0.3 collective-permute-done.9.refs_13_
  23.3 0.2 collective-permute-done.8.refs_12_
  23.5 0.0 collective-permute-done.7.refs_7_
  23.5 0.0 collective-permute-done.6.refs_6_
  23.5 0.0 collective-permute-done.5.refs_5_
  23.5 25.2 %shard_map.143 = (f32[48,128]{1,0:T(8,128)}, f32[48,128]{1,0:T(8,128)}, f32[48,128]{1,0:T(8,128)}) custom-call(s32[1,128]{1,0:T(1,128)S(1)} %get-tuple-element.13.refs_0_, s32[8,128]{1,0:T(8,128)S(1)} %get-tuple-element.14.refs_1_, s32[8,128]{1,0:T(8,128)S(1)} %get-tuple-element.15.refs_2_, s32[32,128]{1,0:T(8,128)S(1)} %shard_map.141.refs_3_, ...), custom_call_target="tpu_custom_call" | custom-call | tf_op jit(solution)/shard_map/pallas_call | solution.py:464
  (2 shorter events, 0.0 us)
Async XLA Ops:
  2.4 1.6 %collective-permute-start.3 = (f32[120,128]{1,0:T(8,128)}, f32[120,128]{1,0:T(8,128)S(1)}, u32[]{:S(2)}, u32[]{:S(2)}) collective-permute-start(f32[120,128]{1,0:T(8,128)} %shard_map.142), channel_id=1, source_target_pairs={{0,8},{8,0},{16,24},{24,16},{1,9},{9,1},{17,25},{25,17},{2,10},{10... | collective-permute-start | bytes 184328 | tf_op jit(solution)/shard_map/ppermute | solution.py:374
  4.0 4.4 %copy-start = (s32[2048]{0:T(1024)S(1)}, s32[2048]{0:T(1024)}, u32[]{:S(2)}) copy-start(s32[2048]{0:T(1024)} %param.18) | copy-start | bytes 24580
  4.0 4.4 %copy-start.1 = (f32[2,3,2048]{2,0,1:T(2,128)S(1)}, f32[2,3,2048]{2,0,1:T(2,128)}, u32[]{:S(2)}) copy-start(f32[2,3,2048]{2,0,1:T(2,128)} %param.15) | copy-start | bytes 147460
  4.0 9.6 %collective-permute-start.4 = (f32[120,128]{1,0:T(8,128)S(1)}, f32[120,128]{1,0:T(8,128)S(1)}, u32[]{:S(2)}, u32[]{:S(2)}) collective-permute-start(f32[120,128]{1,0:T(8,128)S(1)} %broadcast_select_fusion), channel_id=1, source_target_pairs={{0,4},{4,0},{1,5},{5,1},{2,6},{6,2},{3,7},{7,3},{8,12},{12,8},{9,1... | collective-permute-start | bytes 184328 | tf_op jit(solution)/shard_map/ppermute | solution.py:374
  8.3 0.7 %copy-start.2 = (s32[1,64]{1,0:T(1,128)S(1)}, s32[1,64]{1,0:T(1,128)}, u32[]{:S(2)}) copy-start(s32[1,64]{1,0:T(1,128)} %own.1) | copy-start | bytes 772
  8.3 0.7 %copy-start.3 = (s32[1,64]{1,0:T(1,128)S(1)}, s32[1,64]{1,0:T(1,128)}, u32[]{:S(2)}) copy-start(s32[1,64]{1,0:T(1,128)} %other.1) | copy-start | bytes 772
  9.3 8.8 %collective-permute-start.2 = (f32[56,128]{1,0:T(8,128)S(1)}, f32[56,128]{1,0:T(8,128)S(1)}, u32[]{:S(2)}, u32[]{:S(2)}) collective-permute-start(f32[56,128]{1,0:T(8,128)S(1)} %get-tuple-element.12), channel_id=1, source_target_pairs={{3,0},{2,1},{1,2},{0,3},{7,4},{6,5},{5,6},{4,7},{11,8},{10,9},{9,1... | collective-permute-start | bytes 86024 | tf_op jit(solution)/shard_map/ppermute | solution.py:380
  13.0 5.8 %collective-permute-start.1 = (f32[56,128]{1,0:T(8,128)S(1)}, f32[56,128]{1,0:T(8,128)S(1)}, u32[]{:S(2)}, u32[]{:S(2)}) collective-permute-start(f32[56,128]{1,0:T(8,128)S(1)} %get-tuple-element.12), channel_id=1, source_target_pairs={{2,0},{3,1},{0,2},{1,3},{6,4},{7,5},{4,6},{5,7},{10,8},{11,9},{8,1... | collective-permute-start | bytes 86024 | tf_op jit(solution)/shard_map/ppermute | solution.py:380
  13.6 9.8 %collective-permute-start.7 = (f32[120,128]{1,0:T(8,128)S(1)}, f32[120,128]{1,0:T(8,128)S(1)}, u32[]{:S(2)}, u32[]{:S(2)}) collective-permute-start(f32[120,128]{1,0:T(8,128)S(1)} %broadcast_select_fusion.1.refs_4_), channel_id=1, source_target_pairs={{3,0},{2,1},{1,2},{0,3},{7,4},{6,5},{5,6},{4,7},{11,8},{10,9},{9,1... | collective-permute-start | bytes 184328 | tf_op jit(solution)/shard_map/ppermute | solution.py:380
  15.6 7.9 %collective-permute-start.6 = (f32[120,128]{1,0:T(8,128)S(1)}, f32[120,128]{1,0:T(8,128)S(1)}, u32[]{:S(2)}, u32[]{:S(2)}) collective-permute-start(f32[120,128]{1,0:T(8,128)S(1)} %broadcast_select_fusion.1.refs_4_), channel_id=1, source_target_pairs={{2,0},{3,1},{0,2},{1,3},{6,4},{7,5},{4,6},{5,7},{10,8},{11,9},{8,1... | collective-permute-start | bytes 184328 | tf_op jit(solution)/shard_map/ppermute | solution.py:380
  16.7 6.8 %collective-permute-start.5 = (f32[120,128]{1,0:T(8,128)S(1)}, f32[120,128]{1,0:T(8,128)S(1)}, u32[]{:S(2)}, u32[]{:S(2)}) collective-permute-start(f32[120,128]{1,0:T(8,128)S(1)} %broadcast_select_fusion.1.refs_4_), channel_id=1, source_target_pairs={{1,0},{0,1},{3,2},{2,3},{5,4},{4,5},{7,6},{6,7},{9,8},{8,9},{11,10... | collective-permute-start | bytes 184328 | tf_op jit(solution)/shard_map/ppermute | solution.py:380
  18.1 4.0 %collective-permute-start = (f32[56,128]{1,0:T(8,128)S(1)}, f32[56,128]{1,0:T(8,128)S(1)}, u32[]{:S(2)}, u32[]{:S(2)}) collective-permute-start(f32[56,128]{1,0:T(8,128)S(1)} %get-tuple-element.12), channel_id=1, source_target_pairs={{1,0},{0,1},{3,2},{2,3},{5,4},{4,5},{7,6},{6,7},{9,8},{8,9},{11,10... | collective-permute-start | bytes 86024 | tf_op jit(solution)/shard_map/ppermute | solution.py:380
  18.7 3.4 %collective-permute-start.10 = (f32[56,128]{1,0:T(8,128)S(1)}, f32[56,128]{1,0:T(8,128)S(1)}, u32[]{:S(2)}, u32[]{:S(2)}) collective-permute-start(f32[56,128]{1,0:T(8,128)S(1)} %collective-permute-done.2.refs_3_.refs_11_), channel_id=1, source_target_pairs={{0,8},{8,0},{16,24},{24,16},{1,9},{9,1},{17,25},{25,17},{2,10},{10... | collective-permute-start | bytes 86024 | tf_op jit(solution)/shard_map/ppermute | solution.py:451
  22.1 1.2 %collective-permute-start.9 = (f32[56,128]{1,0:T(8,128)S(1)}, f32[56,128]{1,0:T(8,128)S(1)}, u32[]{:S(2)}, u32[]{:S(2)}) collective-permute-start(f32[56,128]{1,0:T(8,128)S(1)} %collective-permute-done.1.refs_2_.refs_10_), channel_id=1, source_target_pairs={{0,8},{8,0},{16,24},{24,16},{1,9},{9,1},{17,25},{25,17},{2,10},{10... | collective-permute-start | bytes 86024 | tf_op jit(solution)/shard_map/ppermute | solution.py:451
  22.1 1.4 %collective-permute-start.8 = (f32[56,128]{1,0:T(8,128)S(1)}, f32[56,128]{1,0:T(8,128)S(1)}, u32[]{:S(2)}, u32[]{:S(2)}) collective-permute-start(f32[56,128]{1,0:T(8,128)S(1)} %collective-permute-done.refs_1_.refs_9_), channel_id=1, source_target_pairs={{0,8},{8,0},{16,24},{24,16},{1,9},{9,1},{17,25},{25,17},{2,10},{10... | collective-permute-start | bytes 86024 | tf_op jit(solution)/shard_map/ppermute | solution.py:451
